TPU v7x, 32 devices: a whole 2x2x4 slice. The times are simulated.
32 devices in a mesh: parts: 2 (over x), row: 16 (over z, y, core).
Axes of the slice: x: 2, y: 2, z: 4, core: 2. Of those that a mesh axis runs over, the one named last changes fastest.
Arguments:
- sigma_top: bfloat16 [4096, 2048], P(('parts', 'row')), parts along dimension 0, may hold values from -2 to 8, as said below
- panel_par: bfloat16 [4096, 1024], P(('parts', 'row')), parts along dimension 0, may hold values from -0.25 to 0.25
- dinv_par: float32 [2048, 1024], P(('parts', 'row')), parts along dimension 0, may hold values from -2 to 8, as said below
- panel_kid_top: bfloat16 [4, 2048, 1024], P('parts', 'row'), parts along dimension 0, may hold values from -0.25 to 0.25
- panel_kid_par: bfloat16 [4, 1024, 1024], P('parts', 'row'), parts along dimension 0, may hold values from -0.375 to 0.375
- dvar_kid: float32 [4, 1024], P('parts'), parts along dimension 0, may hold values from 0.5 to 2
- mask_par: int32 [16, 4], P('parts'), parts along dimension 0, may hold values 0 or 1
- mask_kid_top: int32 [4, 8, 4], P('parts'), parts along dimension 0, may hold values 0 or 1
- mask_kid_par: int32 [4, 4, 4], P('parts'), parts along dimension 0, may hold values 0 or 1
Outputs:
- cross_par: bfloat16 [4096, 1024], P(('parts', 'row')), parts along dimension 0
- sigma_par: bfloat16 [2048, 1024], P(('parts', 'row')), parts along dimension 0
- cross_kid_top: bfloat16 [4, 2048, 1024], P('parts', 'row'), parts along dimension 0
- cross_kid_par: bfloat16 [4, 1024, 1024], P('parts', 'row'), parts along dimension 0
- variance_kid: float32 [4, 1024], P('parts'), parts along dimension 0
There are 2 independent parts, one for each index of `parts`. A program takes and returns all parts, laid end to end along the dimension named above; each array names one. Nothing has to cross between parts.
Inputs may be any that keep to these rules, and one draw needn't show every extreme that they name: `sigma_top`: symmetric positive definite. `dinv_par`: symmetric positive definite.
All inputs are finite; a program needn't handle non-finite values.
Results may differ from a plain program's by a relative error of at most 0.0052.
Values may be sent and summed in bfloat16 or wider, within the bound.
A program may use at most 64 MiB of HBM per device.

v0:
```python
import jax
import jax.numpy as jnp
from jax import lax
from jax.sharding import PartitionSpec as P

BLK = 256


def block_mask(mask, rows, first):
    index = (first + jnp.arange(rows, dtype=jnp.int32)) // BLK
    picker = (index[:, None] == jnp.arange(mask.shape[-2], dtype=jnp.int32)[None, :]).astype(
        jnp.float32
    )
    picked = jnp.einsum("rb,...bc->...rc", picker, mask.astype(jnp.float32))
    return jnp.repeat(picked, BLK, axis=-1).astype(jnp.bfloat16)


def shards(
    sigma_top,
    panel_par,
    dinv_par,
    panel_kid_top,
    panel_kid_par,
    dvar_kid,
    mask_par,
    mask_kid_top,
    mask_kid_par,
):
    rows_top = sigma_top.shape[0]
    rows_par = dinv_par.shape[0]
    position = lax.axis_index("row")
    par_masked = panel_par * block_mask(mask_par, rows_top, position * rows_top)
    kid_top_masked = panel_kid_top * block_mask(mask_kid_top, rows_top, position * rows_top)
    kid_par_masked = panel_kid_par * block_mask(mask_kid_par, rows_par, position * rows_par)
    columns = sigma_top
    cross_wide = jnp.dot(
        columns,
        lax.all_gather(par_masked, "row", axis=0, tiled=True),
        preferred_element_type=jnp.float32,
    )
    cross_par = cross_wide.astype(jnp.bfloat16)
    turned = lax.all_to_all(par_masked, "row", split_axis=1, concat_axis=0, tiled=True)
    panel_rows = turned.T
    columns = panel_rows
    diag_sum = jnp.dot(
        columns,
        lax.all_gather(cross_par, "row", axis=0, tiled=True),
        preferred_element_type=jnp.float32,
    )
    sigma_par = (dinv_par + diag_sum).astype(jnp.bfloat16)
    turned_cross = lax.all_to_all(cross_par, "row", split_axis=1, concat_axis=0, tiled=True)
    cross_rows_par = turned_cross.T
    piece = lax.all_gather(kid_top_masked, "row", axis=1, tiled=True)
    upper = jnp.einsum("rc,kcw->krw", sigma_top, piece, preferred_element_type=jnp.float32)
    lower = jnp.einsum("rc,kcw->krw", cross_rows_par, piece, preferred_element_type=jnp.float32)
    acc_top = upper
    acc_par = lower
    piece = lax.all_gather(kid_par_masked, "row", axis=1, tiled=True)
    upper = acc_top + jnp.einsum(
        "rc,kcw->krw", cross_par, piece, preferred_element_type=jnp.float32
    )
    lower = acc_par + jnp.einsum(
        "rc,kcw->krw", sigma_par, piece, preferred_element_type=jnp.float32
    )
    cross_kid_top = upper.astype(jnp.bfloat16)
    cross_kid_par = lower.astype(jnp.bfloat16)
    partial_var = jnp.sum(
        kid_top_masked.astype(jnp.float32) * cross_kid_top.astype(jnp.float32), axis=1
    )
    partial_var = partial_var + jnp.sum(
        kid_par_masked.astype(jnp.float32) * cross_kid_par.astype(jnp.float32), axis=1
    )
    variance_kid = dvar_kid + lax.psum(partial_var, "row")
    return (cross_par, sigma_par, cross_kid_top, cross_kid_par, variance_kid)


def solution(mesh):
    return jax.shard_map(
        shards,
        mesh=mesh,
        in_specs=(
            P(("parts", "row"), None),
            P(("parts", "row"), None),
            P(("parts", "row"), None),
            P("parts", "row", None),
            P("parts", "row", None),
            P("parts", None),
            P("parts", None),
            P("parts", None, None),
            P("parts", None, None),
        ),
        out_specs=(
            P(("parts", "row"), None),
            P(("parts", "row"), None),
            P("parts", "row", None),
            P("parts", "row", None),
            P("parts", None),
        ),
        check_vma=False,
    )
```

profile of v0, /device:TPU:0, one launch (start us, length us, event | category | flops | bytes accessed | tf_op | source)
XLA Modules:
  0.0 304.0 jit_solution(11202252859310362242)
XLA Ops:
  7.2 0.0 copy-start
  7.2 0.0 all-gather.5.cloned.1.call-start
  7.3 1.2 copy.21
  8.4 0.8 convolution_convert_fusion.1
  9.2 0.7 bitcast_multiply_fusion
  10.0 0.0 all-gather.5.cloned.1.call-update
  10.0 0.0 copy-start.5
  10.0 0.0 copy-start.11
  10.0 0.0 copy-start.7
  10.0 0.0 all-gather.7.cloned.1.call-start
  10.1 55.9 %all-gather.5.cloned.1.call-done = bf16[2048,1024]{0,1:T(8,128)(2,1)} async-done(((bf16[128,1024]{0,1:T(8,128)(2,1)}), bf16[2048,1024]{0,1:T(8,128)(2,1)}) %all-gather.5.cloned.1.call-update) | async-done | bytes 4194320 | tf_op jit(solution)/shard_map/all_gather | solution.py:38
  66.0 4.1 %convolution_convert_fusion = bf16[1024,128]{1,0:T(8,128)(2,1)} fusion(bf16[2048,1024]{0,1:T(8,128)(2,1)} %all-gather.5.cloned.1.call-done, bf16[128,2048]{1,0:T(8,128)(2,1)S(1)} %copy-done), kind=kOutput, calls=%fused_computation.5 | convolution fusion | flops 537001984 | bytes 4980736 | tf_op jit(solution)/shard_map/dot_general | solution.py:36
  70.1 0.0 all-gather.7.cloned.1.call-update
  70.1 0.0 all-gather.9.cloned.1.call-start
  70.2 0.0 copy-start.8
  70.2 0.1 fusion.12
  70.3 0.1 copy.23
  70.5 0.3 broadcast_in_dim.7
  70.8 0.4 convert_element_type.81
  71.2 1.0 mul.24
  72.2 0.0 all-gather.9.cloned.1.call-update
  72.2 0.0 all-gather.11.cloned.1.call-start
  72.3 0.1 copy.24
  72.4 0.1 fusion.16
  72.6 0.1 copy.25
  72.7 0.2 broadcast_in_dim.8
  72.9 0.2 convert_element_type.85
  73.1 0.0 copy-done.7
  73.1 0.8 mul.26
  73.8 0.0 all-gather.11.cloned.1.call-update
  73.9 16.0 %all_to_all.38 = bf16[128,16,64]{0,2,1:T(8,128)(2,1)S(1)} all-to-all(bf16[128,16,64]{0,2,1:T(8,128)(2,1)S(1)} %bitcast.55), channel_id=1, replica_groups=mesh['parts'=2,'row'=16] {'row'}, dimensions={1} | all-to-all | bytes 524288 | tf_op jit(solution)/shard_map/all_to_all | solution.py:51
  89.9 5.7 %all-to-all-start = ((bf16[128,16,64]{0,2,1:T(8,128)(2,1)}), bf16[128,16,64]{0,2,1:T(8,128)(2,1)S(1)}, u32[]{:S(2)}, u32[]{:S(2)}) async-start(bf16[128,16,64]{0,2,1:T(8,128)(2,1)} %bitcast.2), calls=%async_computation | async-start | bytes 524288 | tf_op jit(solution)/shard_map/all_to_all | solution.py:42
  95.6 0.8 copy.28
  96.5 0.2 copy.27
  96.6 0.1 reshape.66
  96.8 9.4 %all-to-all-done = bf16[128,16,64]{0,2,1:T(8,128)(2,1)S(1)} async-done(((bf16[128,16,64]{0,2,1:T(8,128)(2,1)}), bf16[128,16,64]{0,2,1:T(8,128)(2,1)S(1)}, u32[]{:S(2)}, u32[]{:S(2)}) %all-to-all-start) | async-done | bytes 262176 | tf_op jit(solution)/shard_map/all_to_all | solution.py:42
  106.1 21.0 %all-gather.7.cloned.1.call-done = bf16[2048,1024]{0,1:T(8,128)(2,1)} async-done(((bf16[128,1024]{0,1:T(8,128)(2,1)}), bf16[2048,1024]{0,1:T(8,128)(2,1)}) %all-gather.7.cloned.1.call-update) | async-done | bytes 4194320 | tf_op jit(solution)/shard_map/all_gather | solution.py:47
  127.2 3.6 %fusion.4 = bf16[64,1024]{1,0:T(8,128)(2,1)S(1)} fusion(f32[64,1024]{1,0:T(8,128)S(1)} %copy-done.8, bf16[2048,1024]{0,1:T(8,128)(2,1)} %all-gather.7.cloned.1.call-done, bf16[128,16,64]{0,2,1:T(8,128)(2,1)S(1)} %all-to-all-done), kind=kOutput, calls=%fused_computation.8 | convolution fusion | flops 268566528 | bytes 4849664 | tf_op jit(solution)/shard_map/dot_general | solution.py:45
  130.8 73.5 %all-gather.9.cloned.1.call-done = bf16[2,2048,1024]{2,1,0:T(8,128)(2,1)} async-done(((bf16[2,128,1024]{2,1,0:T(8,128)(2,1)}), bf16[2,2048,1024]{2,1,0:T(8,128)(2,1)}) %all-gather.9.cloned.1.call-update) | async-done | bytes 8388624 | tf_op jit(solution)/shard_map/all_gather | solution.py:53
  204.3 4.6 %fusion.5 = f32[2,1024,128]{1,2,0:T(8,128)S(1)} fusion(bf16[2,2048,1024]{2,1,0:T(8,128)(2,1)} %all-gather.9.cloned.1.call-done, bf16[128,2048]{1,0:T(8,128)(2,1)S(1)} %copy-done), kind=kOutput, calls=%fused_computation.11 | convolution fusion | flops 1073741824 | bytes 9961472 | tf_op jit(solution)/shard_map/rc,kcw->krw/dot_general | solution.py:54
  208.9 0.0 copy-start.2
  209.0 46.4 %all-gather.11.cloned.1.call-done = bf16[2,1024,1024]{2,1,0:T(8,128)(2,1)} async-done(((bf16[2,64,1024]{2,1,0:T(8,128)(2,1)}), bf16[2,1024,1024]{2,1,0:T(8,128)(2,1)}) %all-gather.11.cloned.1.call-update) | async-done | bytes 4194320 | tf_op jit(solution)/shard_map/all_gather | solution.py:58
  255.4 3.2 %fusion.10 = f32[2,1024,64]{1,2,0:T(8,128)S(1)} fusion(bf16[2,1024,1024]{2,1,0:T(8,128)(2,1)} %all-gather.11.cloned.1.call-done, bf16[64,1024]{1,0:T(8,128)(2,1)S(1)} %fusion.4), kind=kOutput, calls=%fused_computation.18 | convolution fusion | flops 268435456 | bytes 4849664 | tf_op jit(solution)/shard_map/rc,kcw->krw/dot_general | solution.py:62
  258.6 4.2 %multiply_reduce_fusion = (f32[2,1024]{1,0:T(2,128)S(1)}, bf16[2,128,1024]{2,1,0:T(8,128)(2,1)}) fusion(bf16[2,128,1024]{2,1,0:T(8,128)(2,1)S(1)} %copy-done.2, f32[2,1024,128]{1,2,0:T(8,128)S(1)} %fusion.5, bf16[2,1024,1024]{2,1,0:T(8,128)(2,1)} %all-gather.11.cloned.1.call-done, bf16[1024,128]{1,0:T(8,128)(2,1)S(1)} %copy-done.4), kind=kOutput, calls=%fused_computation.10 | convolution fusion | flops 538441728 | bytes 6561792 | tf_op jit(solution)/shard_map/rc,kcw->krw/dot_general | solution.py:59
  262.8 0.0 copy-start.9
  262.8 2.3 multiply_reduce_fusion.1
  265.1 31.7 %psum.7 = f32[2,1024]{1,0:T(2,128)S(1)} all-reduce(f32[2,1024]{1,0:T(2,128)S(1)} %add.58), channel_id=1, replica_groups=mesh['parts'=2,'row'=16] {'row'}, use_global_device_ids=true, to_apply=%region_2.3 | all-reduce | flops 2048 | bytes 16384 | tf_op jit(solution)/shard_map/psum | solution.py:73
  296.8 0.6 add.59
  (23 shorter events, 0.1 us)
Async XLA Ops:
  7.2 58.8 %copy-start = (bf16[128,2048]{1,0:T(8,128)(2,1)S(1)}, bf16[128,2048]{1,0:T(8,128)(2,1)}, u32[]{:S(2)}) copy-start(bf16[128,2048]{1,0:T(8,128)(2,1)} %param.9) | copy-start | bytes 1572868
  7.2 63.0 %copy-start.10 = (s32[2,8,4]{1,2,0:T(4,128)S(1)}, s32[2,8,4]{1,2,0:T(4,128)}, u32[]{:S(2)}) copy-start(s32[2,8,4]{1,2,0:T(4,128)} %param.16) | copy-start | bytes 772
  7.2 58.8 %all-gather.5.cloned.1.call-start = ((), (), s32[]{:S(2)}) async-start(), calls=%async_computation.2 | async-start | bytes 4456448 | tf_op jit(solution)/shard_map/all_gather | solution.py:38
  10.0 61.2 %copy-start.5 = (bf16[2,128,1024]{2,1,0:T(8,128)(2,1)S(1)}, bf16[2,128,1024]{2,1,0:T(8,128)(2,1)}, u32[]{:S(2)}) copy-start(bf16[2,128,1024]{2,1,0:T(8,128)(2,1)} %param.12) | copy-start | bytes 1572868
  10.0 62.3 %copy-start.11 = (s32[2,4,4]{2,1,0:T(4,128)S(1)}, s32[2,4,4]{2,1,0:T(4,128)}, u32[]{:S(2)}) copy-start(s32[2,4,4]{2,1,0:T(4,128)} %param.17) | copy-start | bytes 388
  10.0 63.1 %copy-start.7 = (bf16[2,64,1024]{2,1,0:T(8,128)(2,1)S(1)}, bf16[2,64,1024]{2,1,0:T(8,128)(2,1)}, u32[]{:S(2)}) copy-start(bf16[2,64,1024]{2,1,0:T(8,128)(2,1)} %param.13) | copy-start | bytes 786436
  10.0 117.2 %all-gather.7.cloned.1.call-start = ((), (), s32[]{:S(2)}) async-start(), calls=%async_computation.3 | async-start | bytes 4456448 | tf_op jit(solution)/shard_map/all_gather | solution.py:47
  70.1 3.8 %copy-start.4 = (bf16[1024,128]{1,0:T(8,128)(2,1)S(1)}, bf16[1024,128]{1,0:T(8,128)(2,1)}, u32[]{:S(2)}) copy-start(bf16[1024,128]{1,0:T(8,128)(2,1)} %convolution_convert_fusion) | copy-start | bytes 786436
  70.1 134.2 %all-gather.9.cloned.1.call-start = ((), (), s32[]{:S(2)}) async-start(), calls=%async_computation.4 | async-start | bytes 8912896 | tf_op jit(solution)/shard_map/all_gather | solution.py:53
  70.2 57.0 %copy-start.8 = (f32[64,1024]{1,0:T(8,128)S(1)}, f32[64,1024]{1,0:T(8,128)}, u32[]{:S(2)}) copy-start(f32[64,1024]{1,0:T(8,128)} %param.11) | copy-start | bytes 786436
  72.2 183.1 %all-gather.11.cloned.1.call-start = ((), (), s32[]{:S(2)}) async-start(), calls=%async_computation.5 | async-start | bytes 4456448 | tf_op jit(solution)/shard_map/all_gather | solution.py:58
  89.9 16.3 %all-to-all-start = ((bf16[128,16,64]{0,2,1:T(8,128)(2,1)}), bf16[128,16,64]{0,2,1:T(8,128)(2,1)S(1)}, u32[]{:S(2)}, u32[]{:S(2)}) async-start(bf16[128,16,64]{0,2,1:T(8,128)(2,1)} %bitcast.2), calls=%async_computation | async-start | bytes 524288 | tf_op jit(solution)/shard_map/all_to_all | solution.py:42
  130.8 124.6 %copy-start.6 = (bf16[64,1024]{1,0:T(8,128)(2,1)}, bf16[64,1024]{1,0:T(8,128)(2,1)S(1)}, u32[]{:S(2)}) copy-start(bf16[64,1024]{1,0:T(8,128)(2,1)S(1)} %fusion.4) | copy-start | bytes 393220
  208.9 49.6 %copy-start.2 = (bf16[2,128,1024]{2,1,0:T(8,128)(2,1)S(1)}, bf16[2,128,1024]{2,1,0:T(8,128)(2,1)}, u32[]{:S(2)}) copy-start(bf16[2,128,1024]{2,1,0:T(8,128)(2,1)} %mul.24) | copy-start | bytes 1572868
  255.4 7.4 %copy-start.1 = (bf16[2,2048,1024]{2,1,0:T(8,128)(2,1)S(1)}, bf16[2,2048,1024]{2,1,0:T(8,128)(2,1)}, u32[]{:S(2)}) copy-start(bf16[2,2048,1024]{2,1,0:T(8,128)(2,1)} %all-gather.9.cloned.1.call-done) | copy-start | bytes 25165828
  258.6 4.3 %copy-start.3 = (bf16[2,64,1024]{2,1,0:T(8,128)(2,1)S(1)}, bf16[2,64,1024]{2,1,0:T(8,128)(2,1)}, u32[]{:S(2)}) copy-start(bf16[2,64,1024]{2,1,0:T(8,128)(2,1)} %mul.26) | copy-start | bytes 786436
  262.8 34.0 %copy-start.9 = (f32[2,1024]{1,0:T(2,128)S(1)}, f32[2,1024]{1,0:T(2,128)}, u32[]{:S(2)}) copy-start(f32[2,1024]{1,0:T(2,128)} %param.14) | copy-start | bytes 24580
Sparse Core Ops, SparseCore 0:
  10.7 55.1 all-gather.4
  70.2 56.9 all-gather.6
  130.0 74.2 all-gather.8
  206.3 48.9 all-gather.10
where the time goes:
time: 304 us
  waiting for transfers between devices  206 us (68%)
  blocking collectives  47.7 us (16%)
  matrix products  23.1 us (8%)
  between operations  14 us (5%)
  starting transfers between devices  5.89 us (2%)
  local copies, waits for them, and re-layouts  3.83 us (1%)
  other arithmetic  3.14 us (1%)
    all_gather x1, waiting for transfers between devices, shards(): piece = lax.all_gather(kid_top_masked, 'row', axis=1, tiled=True)  73.5 us
    all_gather x1, waiting for transfers between devices, shards(): lax.all_gather(par_masked, 'row', axis=0, tiled=True)  55.9 us
    all_gather x1, waiting for transfers between devices, shards(): piece = lax.all_gather(kid_par_masked, 'row', axis=1, tiled=True)  46.4 us
    psum x1, blocking collectives, shards(): variance_kid = dvar_kid + lax.psum(partial_var, 'row')  31.7 us
    all_gather x1, waiting for transfers between devices, shards(): lax.all_gather(cross_par, 'row', axis=0, tiled=True)  21 us
    all_to_all x1, blocking collectives, shards(): lax.all_to_all(cross_par, 'row', split_axis=1, concat_axis=0, tiled=True)  16 us
    all_to_all x1, waiting for transfers between devices, shards(): lax.all_to_all(par_masked, 'row', split_axis=1, concat_axis=0, tiled=True)  9.39 us
  transfers between devices with their start and end apart: 5, of which 5 were waited for; matrix products, arithmetic and copies ran while one was open for 4% of the time, Pallas kernels for 0%

commit v1 on v0

--- a/solution.py
+++ b/solution.py
@@ -70,7 +70,7 @@
     partial_var = partial_var + jnp.sum(
         kid_par_masked.astype(jnp.float32) * cross_kid_par.astype(jnp.float32), axis=1
     )
-    variance_kid = dvar_kid + lax.psum(partial_var, "row")
+    variance_kid = dvar_kid + jnp.sum(lax.all_gather(partial_var, "row"), axis=0)
     return (cross_par, sigma_par, cross_kid_top, cross_kid_par, variance_kid)
 
 

time: 304 us -> 292 us (0.961)
  blocking collectives: 47.7 us -> 35.3 us
    psum x1 -> x0, blocking collectives: 31.7 us -> none  [shards(): variance_kid = dvar_kid + lax.psum(partial_var, 'row')]
    all_gather x0 -> x1, blocking collectives: none -> 19.3 us  [shards(): lax.all_gather(partial_var, 'row')]
where the time goes in v1:
time: 292 us
  waiting for transfers between devices  206 us (71%)
  blocking collectives  35.3 us (12%)
  matrix products  23.1 us (8%)
  between operations  14 us (5%)
  starting transfers between devices  5.89 us (2%)
  local copies, waits for them, and re-layouts  3.83 us (1%)
  other arithmetic  3.2 us (1%)
    all_gather x1, waiting for transfers between devices, shards(): piece = lax.all_gather(kid_top_masked, 'row', axis=1, tiled=True)  73.5 us
    all_gather x1, waiting for transfers between devices, shards(): lax.all_gather(par_masked, 'row', axis=0, tiled=True)  55.9 us
    all_gather x1, waiting for transfers between devices, shards(): piece = lax.all_gather(kid_par_masked, 'row', axis=1, tiled=True)  46.4 us
    all_gather x1, waiting for transfers between devices, shards(): lax.all_gather(cross_par, 'row', axis=0, tiled=True)  21 us
    all_gather x1, blocking collectives, shards(): lax.all_gather(partial_var, 'row')  19.3 us
    all_to_all x1, blocking collectives, shards(): lax.all_to_all(cross_par, 'row', split_axis=1, concat_axis=0, tiled=True)  16 us
    all_to_all x1, waiting for transfers between devices, shards(): lax.all_to_all(par_masked, 'row', split_axis=1, concat_axis=0, tiled=True)  9.39 us
  transfers between devices with their start and end apart: 5, of which 5 were waited for; matrix products, arithmetic and copies ran while one was open for 4% of the time, Pallas kernels for 0%

profile of v1, /device:TPU:0, one launch (start us, length us, event | category | flops | bytes accessed | tf_op | source)
XLA Modules:
  0.0 291.6 jit_solution(232374125042991005)
XLA Ops:
  7.2 0.0 copy-start
  7.2 0.0 all-gather.7.cloned.1.call-start
  7.3 1.2 copy.29
  8.4 0.8 convolution_convert_fusion.1
  9.2 0.7 bitcast_multiply_fusion
  10.0 0.0 all-gather.7.cloned.1.call-update
  10.0 0.0 copy-start.5
  10.0 0.0 copy-start.11
  10.0 0.0 copy-start.7
  10.0 0.0 all-gather.9.cloned.1.call-start
  10.1 55.9 %all-gather.7.cloned.1.call-done = bf16[2048,1024]{0,1:T(8,128)(2,1)} async-done(((bf16[128,1024]{0,1:T(8,128)(2,1)}), bf16[2048,1024]{0,1:T(8,128)(2,1)}) %all-gather.7.cloned.1.call-update) | async-done | bytes 4194320 | tf_op jit(solution)/shard_map/all_gather | solution.py:38
  66.0 4.1 %convolution_convert_fusion = bf16[1024,128]{1,0:T(8,128)(2,1)} fusion(bf16[2048,1024]{0,1:T(8,128)(2,1)} %all-gather.7.cloned.1.call-done, bf16[128,2048]{1,0:T(8,128)(2,1)S(1)} %copy-done), kind=kOutput, calls=%fused_computation.5 | convolution fusion | flops 537001984 | bytes 4980736 | tf_op jit(solution)/shard_map/dot_general | solution.py:36
  70.1 0.0 all-gather.9.cloned.1.call-update
  70.1 0.0 all-gather.11.cloned.1.call-start
  70.2 0.0 copy-start.8
  70.2 0.1 fusion.12
  70.3 0.1 copy.31
  70.5 0.3 broadcast_in_dim.7
  70.8 0.4 convert_element_type.81
  71.2 1.0 mul.24
  72.2 0.0 all-gather.11.cloned.1.call-update
  72.2 0.0 all-gather.13.cloned.1.call-start
  72.3 0.1 copy.32
  72.4 0.1 fusion.16
  72.6 0.1 copy.33
  72.7 0.2 broadcast_in_dim.8
  72.9 0.2 convert_element_type.85
  73.1 0.8 mul.26
  73.8 0.0 all-gather.13.cloned.1.call-update
  73.9 16.0 %all_to_all.38 = bf16[128,16,64]{0,2,1:T(8,128)(2,1)S(1)} all-to-all(bf16[128,16,64]{0,2,1:T(8,128)(2,1)S(1)} %bitcast.57), channel_id=1, replica_groups=mesh['parts'=2,'row'=16] {'row'}, dimensions={1} | all-to-all | bytes 524288 | tf_op jit(solution)/shard_map/all_to_all | solution.py:51
  89.9 5.7 %all-to-all-start = ((bf16[128,16,64]{0,2,1:T(8,128)(2,1)}), bf16[128,16,64]{0,2,1:T(8,128)(2,1)S(1)}, u32[]{:S(2)}, u32[]{:S(2)}) async-start(bf16[128,16,64]{0,2,1:T(8,128)(2,1)} %bitcast.2), calls=%async_computation | async-start | bytes 524288 | tf_op jit(solution)/shard_map/all_to_all | solution.py:42
  95.6 0.8 copy.36
  96.5 0.2 copy.35
  96.6 0.1 reshape.82
  96.8 9.4 %all-to-all-done = bf16[128,16,64]{0,2,1:T(8,128)(2,1)S(1)} async-done(((bf16[128,16,64]{0,2,1:T(8,128)(2,1)}), bf16[128,16,64]{0,2,1:T(8,128)(2,1)S(1)}, u32[]{:S(2)}, u32[]{:S(2)}) %all-to-all-start) | async-done | bytes 262176 | tf_op jit(solution)/shard_map/all_to_all | solution.py:42
  106.1 21.0 %all-gather.9.cloned.1.call-done = bf16[2048,1024]{0,1:T(8,128)(2,1)} async-done(((bf16[128,1024]{0,1:T(8,128)(2,1)}), bf16[2048,1024]{0,1:T(8,128)(2,1)}) %all-gather.9.cloned.1.call-update) | async-done | bytes 4194320 | tf_op jit(solution)/shard_map/all_gather | solution.py:47
  127.2 3.6 %fusion.4 = bf16[64,1024]{1,0:T(8,128)(2,1)S(1)} fusion(f32[64,1024]{1,0:T(8,128)S(1)} %copy-done.8, bf16[2048,1024]{0,1:T(8,128)(2,1)} %all-gather.9.cloned.1.call-done, bf16[128,16,64]{0,2,1:T(8,128)(2,1)S(1)} %all-to-all-done), kind=kOutput, calls=%fused_computation.8 | convolution fusion | flops 268566528 | bytes 4849664 | tf_op jit(solution)/shard_map/dot_general | solution.py:45
  130.8 73.5 %all-gather.11.cloned.1.call-done = bf16[2,2048,1024]{2,1,0:T(8,128)(2,1)} async-done(((bf16[2,128,1024]{2,1,0:T(8,128)(2,1)}), bf16[2,2048,1024]{2,1,0:T(8,128)(2,1)}) %all-gather.11.cloned.1.call-update) | async-done | bytes 8388624 | tf_op jit(solution)/shard_map/all_gather | solution.py:53
  204.3 4.6 %fusion.5 = f32[2,1024,128]{1,2,0:T(8,128)S(1)} fusion(bf16[2,2048,1024]{2,1,0:T(8,128)(2,1)} %all-gather.11.cloned.1.call-done, bf16[128,2048]{1,0:T(8,128)(2,1)S(1)} %copy-done), kind=kOutput, calls=%fused_computation.11 | convolution fusion | flops 1073741824 | bytes 9961472 | tf_op jit(solution)/shard_map/rc,kcw->krw/dot_general | solution.py:54
  208.9 0.0 copy-start.2
  209.0 46.4 %all-gather.13.cloned.1.call-done = bf16[2,1024,1024]{2,1,0:T(8,128)(2,1)} async-done(((bf16[2,64,1024]{2,1,0:T(8,128)(2,1)}), bf16[2,1024,1024]{2,1,0:T(8,128)(2,1)}) %all-gather.13.cloned.1.call-update) | async-done | bytes 4194320 | tf_op jit(solution)/shard_map/all_gather | solution.py:58
  255.4 3.2 %fusion.10 = f32[2,1024,64]{1,2,0:T(8,128)S(1)} fusion(bf16[2,1024,1024]{2,1,0:T(8,128)(2,1)} %all-gather.13.cloned.1.call-done, bf16[64,1024]{1,0:T(8,128)(2,1)S(1)} %fusion.4), kind=kOutput, calls=%fused_computation.18 | convolution fusion | flops 268435456 | bytes 4849664 | tf_op jit(solution)/shard_map/rc,kcw->krw/dot_general | solution.py:62
  258.6 4.2 %multiply_reduce_fusion = (f32[2,1024]{1,0:T(2,128)S(1)}, bf16[2,128,1024]{2,1,0:T(8,128)(2,1)}) fusion(bf16[2,128,1024]{2,1,0:T(8,128)(2,1)S(1)} %copy-done.2, f32[2,1024,128]{1,2,0:T(8,128)S(1)} %fusion.5, bf16[2,1024,1024]{2,1,0:T(8,128)(2,1)} %all-gather.13.cloned.1.call-done, bf16[1024,128]{1,0:T(8,128)(2,1)S(1)} %copy-done.4), kind=kOutput, calls=%fused_computation.10 | convolution fusion | flops 538441728 | bytes 6561792 | tf_op jit(solution)/shard_map/rc,kcw->krw/dot_general | solution.py:59
  262.8 0.0 copy-start.9
  262.8 2.3 multiply_reduce_fusion.1
  265.1 19.3 %all-gather.1 = f32[16,2,1024]{2,1,0:T(2,128)S(1)} all-gather(f32[1,2,1024]{2,1,0:T(2,128)S(1)} %add_bitcast_fusion), channel_id=2, replica_groups=mesh['parts'=2,'row'=16] {'row'}, dimensions={0}, use_global_device_ids=true | all-gather | bytes 139264 | tf_op jit(solution)/shard_map/all_gather | solution.py:73
  284.4 0.1 reduce_sum.29
  284.5 0.6 add.68
  (24 shorter events, 0.1 us)
Async XLA Ops:
  7.2 58.8 %copy-start = (bf16[128,2048]{1,0:T(8,128)(2,1)S(1)}, bf16[128,2048]{1,0:T(8,128)(2,1)}, u32[]{:S(2)}) copy-start(bf16[128,2048]{1,0:T(8,128)(2,1)} %param.9) | copy-start | bytes 1572868
  7.2 63.0 %copy-start.10 = (s32[2,8,4]{1,2,0:T(4,128)S(1)}, s32[2,8,4]{1,2,0:T(4,128)}, u32[]{:S(2)}) copy-start(s32[2,8,4]{1,2,0:T(4,128)} %param.16) | copy-start | bytes 772
  7.2 58.8 %all-gather.7.cloned.1.call-start = ((), (), s32[]{:S(2)}) async-start(), calls=%async_computation.2 | async-start | bytes 4456448 | tf_op jit(solution)/shard_map/all_gather | solution.py:38
  10.0 61.2 %copy-start.5 = (bf16[2,128,1024]{2,1,0:T(8,128)(2,1)S(1)}, bf16[2,128,1024]{2,1,0:T(8,128)(2,1)}, u32[]{:S(2)}) copy-start(bf16[2,128,1024]{2,1,0:T(8,128)(2,1)} %param.12) | copy-start | bytes 1572868
  10.0 62.3 %copy-start.11 = (s32[2,4,4]{2,1,0:T(4,128)S(1)}, s32[2,4,4]{2,1,0:T(4,128)}, u32[]{:S(2)}) copy-start(s32[2,4,4]{2,1,0:T(4,128)} %param.17) | copy-start | bytes 388
  10.0 63.1 %copy-start.7 = (bf16[2,64,1024]{2,1,0:T(8,128)(2,1)S(1)}, bf16[2,64,1024]{2,1,0:T(8,128)(2,1)}, u32[]{:S(2)}) copy-start(bf16[2,64,1024]{2,1,0:T(8,128)(2,1)} %param.13) | copy-start | bytes 786436
  10.0 117.2 %all-gather.9.cloned.1.call-start = ((), (), s32[]{:S(2)}) async-start(), calls=%async_computation.3 | async-start | bytes 4456448 | tf_op jit(solution)/shard_map/all_gather | solution.py:47
  70.1 3.8 %copy-start.4 = (bf16[1024,128]{1,0:T(8,128)(2,1)S(1)}, bf16[1024,128]{1,0:T(8,128)(2,1)}, u32[]{:S(2)}) copy-start(bf16[1024,128]{1,0:T(8,128)(2,1)} %convolution_convert_fusion) | copy-start | bytes 786436
  70.1 134.2 %all-gather.11.cloned.1.call-start = ((), (), s32[]{:S(2)}) async-start(), calls=%async_computation.4 | async-start | bytes 8912896 | tf_op jit(solution)/shard_map/all_gather | solution.py:53
  70.2 57.0 %copy-start.8 = (f32[64,1024]{1,0:T(8,128)S(1)}, f32[64,1024]{1,0:T(8,128)}, u32[]{:S(2)}) copy-start(f32[64,1024]{1,0:T(8,128)} %param.11) | copy-start | bytes 786436
  72.2 183.1 %all-gather.13.cloned.1.call-start = ((), (), s32[]{:S(2)}) async-start(), calls=%async_computation.5 | async-start | bytes 4456448 | tf_op jit(solution)/shard_map/all_gather | solution.py:58
  89.9 16.3 %all-to-all-start = ((bf16[128,16,64]{0,2,1:T(8,128)(2,1)}), bf16[128,16,64]{0,2,1:T(8,128)(2,1)S(1)}, u32[]{:S(2)}, u32[]{:S(2)}) async-start(bf16[128,16,64]{0,2,1:T(8,128)(2,1)} %bitcast.2), calls=%async_computation | async-start | bytes 524288 | tf_op jit(solution)/shard_map/all_to_all | solution.py:42
  130.8 124.6 %copy-start.6 = (bf16[64,1024]{1,0:T(8,128)(2,1)}, bf16[64,1024]{1,0:T(8,128)(2,1)S(1)}, u32[]{:S(2)}) copy-start(bf16[64,1024]{1,0:T(8,128)(2,1)S(1)} %fusion.4) | copy-start | bytes 393220
  208.9 49.6 %copy-start.2 = (bf16[2,128,1024]{2,1,0:T(8,128)(2,1)S(1)}, bf16[2,128,1024]{2,1,0:T(8,128)(2,1)}, u32[]{:S(2)}) copy-start(bf16[2,128,1024]{2,1,0:T(8,128)(2,1)} %mul.24) | copy-start | bytes 1572868
  255.4 7.4 %copy-start.1 = (bf16[2,2048,1024]{2,1,0:T(8,128)(2,1)S(1)}, bf16[2,2048,1024]{2,1,0:T(8,128)(2,1)}, u32[]{:S(2)}) copy-start(bf16[2,2048,1024]{2,1,0:T(8,128)(2,1)} %all-gather.11.cloned.1.call-done) | copy-start | bytes 25165828
  258.6 4.3 %copy-start.3 = (bf16[2,64,1024]{2,1,0:T(8,128)(2,1)S(1)}, bf16[2,64,1024]{2,1,0:T(8,128)(2,1)}, u32[]{:S(2)}) copy-start(bf16[2,64,1024]{2,1,0:T(8,128)(2,1)} %mul.26) | copy-start | bytes 786436
  262.8 21.7 %copy-start.9 = (f32[2,1024]{1,0:T(2,128)S(1)}, f32[2,1024]{1,0:T(2,128)}, u32[]{:S(2)}) copy-start(f32[2,1024]{1,0:T(2,128)} %param.14) | copy-start | bytes 24580
Sparse Core Ops, SparseCore 0:
  10.7 55.1 all-gather.6
  70.2 56.9 all-gather.8
  130.0 74.2 all-gather.10
  206.3 48.9 all-gather.12
